TPU v7x, 32 devices: a whole 2x2x4 slice. The times are simulated.
32 devices in a mesh: expert: 4 (over z), mp: 8 (over y, x, core).
Axes of the slice: x: 2, y: 2, z: 4, core: 2. Of those that a mesh axis runs over, the one named last changes fastest.
Arguments:
- tokens: bfloat16 [512, 4096], P(('expert', 'mp')), may hold values from -6 to 6
- gain: bfloat16 [4096], replicated, may hold values from 0.5 to 1.5
- expert_ids: int32 [512, 2], P(('expert', 'mp')), may hold values from 0 to 3, all different within a row; in each aligned block of 16 rows (0 to 15, 16 to 31, ...) at most 10 rows name the same one
- gate_num: int32 [512], P(('expert', 'mp')), may hold values from 1 to 1023
- w_gate: bfloat16 [4, 4096, 14336], P('expert', None, 'mp'), may hold values from -0.09375 to 0.09375
- w_up: bfloat16 [4, 4096, 14336], P('expert', None, 'mp'), may hold values from -0.09375 to 0.09375
- w_down: bfloat16 [4, 14336, 4096], P('expert', 'mp'), may hold values from -0.046875 to 0.046875
Outputs:
- mixed_out: bfloat16 [512, 4096], P(('expert', 'mp'))
Inputs may be any that keep to these rules, and one draw needn't show every extreme that they name: `expert_ids`: the 2 ids of a token differ. Within the rows of one device no expert is named more than 10 times, and some expert reaches 10 on some devices.
All inputs are finite; a program needn't handle non-finite values.
Results may differ from a plain program's by a relative error of at most 0.019.
Values may be sent and summed in bfloat16 or wider, within the bound.
A program may use at most 128 MiB of HBM per device.

v0:
```python
import jax
import jax.numpy as jnp
from jax import lax
from jax.sharding import PartitionSpec as P

DENOM = 1024


def rms_normed(tokens, gain):
    values = tokens.astype(jnp.float32)
    inverse = lax.rsqrt(jnp.mean(values * values, axis=1, keepdims=True) + 1e-05)
    return (values * inverse * gain.astype(jnp.float32)).astype(jnp.bfloat16)


def swiglu(row_block, gate_matrix, up_matrix):
    gate_proj = jnp.dot(row_block, gate_matrix, preferred_element_type=jnp.float32)
    up_proj = jnp.dot(row_block, up_matrix, preferred_element_type=jnp.float32)
    return (jax.nn.silu(gate_proj) * up_proj).astype(jnp.bfloat16)


def slot_plan(expert_ids, experts, capacity):
    flat_ids = expert_ids.reshape(-1)
    slot_count = flat_ids.shape[0]
    slot_order = jnp.arange(slot_count, dtype=jnp.int32)
    earlier = (flat_ids[:, None] == flat_ids[None, :]) & (slot_order[None, :] < slot_order[:, None])
    position = jnp.sum(earlier.astype(jnp.int32), axis=1)
    target = flat_ids * capacity + position
    slot_ids = jnp.arange(experts * capacity, dtype=jnp.int32)
    matched = target[None, :] == slot_ids[:, None]
    token_of = slot_order[None, :] // expert_ids.shape[1] + 1
    slot_owner = jnp.sum(jnp.where(matched, token_of, 0), axis=1) - 1
    return (target, slot_owner)


def body(tokens, gain, expert_ids, gate_num, w_gate, w_up, w_down):
    groups = lax.axis_size("expert")
    tok_rows, model_width = tokens.shape
    top_count = expert_ids.shape[1]
    capacity = (5 * tok_rows * top_count + 4 * groups - 1) // (4 * groups)
    normed = rms_normed(tokens, gain)
    target, slot_owner = slot_plan(expert_ids, groups, capacity)
    gate_matrix = w_gate[0]
    up_matrix = w_up[0]
    down_matrix = w_down[0]
    picked = jnp.take(normed, jnp.maximum(slot_owner, 0), axis=0)
    outgoing = jnp.where((slot_owner >= 0)[:, None], picked, jnp.zeros_like(picked))
    received = lax.all_to_all(
        outgoing.reshape(groups, capacity, model_width),
        "expert",
        split_axis=0,
        concat_axis=0,
        tiled=True,
    )
    received = received.reshape(groups * capacity, model_width)
    hidden = swiglu(lax.all_gather(received, "mp", axis=0, tiled=True), gate_matrix, up_matrix)
    summed = lax.psum_scatter(
        jnp.dot(hidden, down_matrix, preferred_element_type=jnp.float32).astype(jnp.bfloat16),
        "mp",
        scatter_dimension=0,
        tiled=True,
    )
    outcome = summed.reshape(groups, capacity, model_width)
    returned = lax.all_to_all(outcome, "expert", split_axis=0, concat_axis=0, tiled=True)
    flat_back = returned.reshape(groups * capacity, model_width)
    chosen = (
        jnp.take(flat_back, target, axis=0)
        .astype(jnp.float32)
        .reshape(tok_rows, top_count, model_width)
    )
    first_share = gate_num.astype(jnp.float32) / DENOM
    mixed_out = (
        chosen[:, 0, :] * first_share[:, None] + chosen[:, 1, :] * (1.0 - first_share)[:, None]
    )
    return mixed_out.astype(jnp.bfloat16)


def solution(mesh):
    in_specs = (
        P(("expert", "mp"), None),
        P(),
        P(("expert", "mp"), None),
        P(("expert", "mp")),
        P("expert", None, "mp"),
        P("expert", None, "mp"),
        P("expert", "mp", None),
    )
    out_specs = P(("expert", "mp"), None)
    return jax.shard_map(body, mesh=mesh, in_specs=in_specs, out_specs=out_specs, check_vma=False)
```

profile of v0, /device:TPU:0, one launch (start us, length us, event | category | flops | bytes accessed | tf_op | source)
XLA Modules:
  0.0 162.3 jit_solution(16366037808898178722)
XLA Ops:
  6.5 0.0 all-gather.2.cloned.1.call-start
  6.5 0.8 copy.20
  7.3 0.1 reshape.157
  7.4 0.2 convert_reduce_fusion
  7.6 0.1 select_reduce_fusion
  7.7 0.1 ge.29
  7.8 0.1 le.31
  7.9 0.7 convert_element_type.30
  8.6 1.0 fusion.15
  9.6 1.0 fusion.17
  10.6 0.7 gather_fusion
  11.4 0.1 gather.13
  11.5 0.1 select_select_fusion
  11.7 20.6 %all_to_all.10 = bf16[4,10,4096]{2,1,0:T(8,128)(2,1)S(1)} all-to-all(bf16[4,10,4096]{2,1,0:T(8,128)(2,1)S(1)} %select_select_fusion), channel_id=1, replica_groups=mesh['expert'=4,'mp'=8] {'expert'}, dimensions={0} | all-to-all | bytes 655360 | tf_op jit(solution)/shard_map/all_to_all | solution.py:47
  32.3 0.9 reshape.158
  33.2 0.0 all-gather.2.cloned.1.call-update
  33.2 0.0 reduce-scatter.2.cloned.1.call-start
  33.2 29.2 %all-gather.2.cloned.1.call-done = bf16[320,4096]{1,0:T(8,128)(2,1)} async-done(((bf16[40,4096]{1,0:T(8,128)(2,1)}), bf16[320,4096]{1,0:T(8,128)(2,1)}) %all-gather.2.cloned.1.call-update) | async-done | bytes 2621456 | tf_op jit(solution)/shard_map/all_gather | solution.py:55
  62.4 0.0 copy-start.1
  62.4 0.0 slice-start
  62.4 0.0 slice-start.1
  62.4 9.7 %fusion.4 = f32[320,1792]{1,0:T(8,128)S(1)} fusion(bf16[320,4096]{1,0:T(8,128)(2,1)} %all-gather.2.cloned.1.call-done, bf16[1,4096,1792]{2,1,0:T(8,128)(2,1)} %param.11), kind=kOutput, calls=%fused_computation.6 | convolution fusion | flops 4697620480 | bytes 19595264 | tf_op jit(solution)/shard_map/dot_general | solution.py:16
  72.2 0.0 copy-done.1
  72.2 0.0 slice-start.2
  72.2 0.0 slice-start.3
  72.2 10.4 %fusion.12 = bf16[320,1792]{1,0:T(8,128)(2,1)S(1)} fusion(bf16[320,4096]{1,0:T(8,128)(2,1)S(1)} %copy-done.1, bf16[1,4096,1792]{2,1,0:T(8,128)(2,1)} %param.12, f32[320,1792]{1,0:T(8,128)S(1)} %fusion.4), kind=kOutput, calls=%fused_computation.10 | convolution fusion | flops 4701061120 | bytes 20742144 | tf_op jit(solution)/shard_map/dot_general | solution.py:17
  82.6 0.0 slice-done
  82.6 0.0 slice-done.1
  82.6 0.0 slice-done.2
  82.6 0.0 slice-done.3
  82.7 6.2 %fusion.6 = bf16[320,4096]{1,0:T(8,128)(2,1)} fusion(bf16[320,1792]{1,0:T(8,128)(2,1)S(1)} %fusion.12, bf16[1,1792,4096]{2,1,0:T(8,128)(2,1)S(1)} %bitcast.39), kind=kOutput, calls=%fused_computation.8 | convolution fusion | flops 4698931200 | bytes 18448384 | tf_op jit(solution)/shard_map/dot_general | solution.py:57
  88.9 0.0 copy-start
  88.9 0.0 copy-start.2
  88.9 0.0 reduce-scatter.2.cloned.1.call-update
  88.9 0.7 copy-done
  89.6 0.1 copy.22
  89.7 0.1 mul.80
  89.8 42.8 %reduce-scatter.2.cloned.1.call-done = bf16[40,4096]{1,0:T(8,128)(2,1)} async-done(((bf16[320,4096]{1,0:T(8,128)(2,1)}), bf16[40,4096]{1,0:T(8,128)(2,1)}) %reduce-scatter.2.cloned.1.call-update) | async-done | bytes 327696 | tf_op jit(solution)/shard_map/reduce_scatter | solution.py:56
  132.6 1.9 %reshape.159 = bf16[4,10,4096]{2,1,0:T(8,128)(2,1)} reshape(bf16[40,4096]{1,0:T(8,128)(2,1)} %reduce-scatter.2.cloned.1.call-done) | data formatting | bytes 655360 | tf_op jit(solution)/shard_map/reshape | solution.py:62
  134.4 4.6 %all-to-all-start.1 = ((bf16[4,10,4096]{2,1,0:T(8,128)(2,1)}), bf16[4,10,4096]{2,1,0:T(8,128)(2,1)S(1)}, u32[]{:S(2)}, u32[]{:S(2)}) async-start(bf16[4,10,4096]{2,1,0:T(8,128)(2,1)} %reshape.159), calls=%async_computation.2 | async-start | bytes 1048576 | tf_op jit(solution)/shard_map/all_to_all | solution.py:63
  139.1 0.1 reduce_sum.32
  139.1 0.1 copy.21
  139.2 0.0 copy-done.2
  139.2 14.1 %all-to-all-done.1 = bf16[4,10,4096]{2,1,0:T(8,128)(2,1)S(1)} async-done(((bf16[4,10,4096]{2,1,0:T(8,128)(2,1)}), bf16[4,10,4096]{2,1,0:T(8,128)(2,1)S(1)}, u32[]{:S(2)}, u32[]{:S(2)}) %all-to-all-start.1) | async-done | bytes 327712 | tf_op jit(solution)/shard_map/all_to_all | solution.py:63
  153.4 0.1 reshape.160
  153.5 0.7 gather_fusion.1
  154.2 0.2 gather.15
  154.4 0.3 fusion.22
  154.7 0.8 fusion.20
  (11 shorter events, 0.1 us)
Async XLA Ops:
  6.5 55.9 %all-gather.2.cloned.1.call-start = ((), (), s32[]{:S(2)}) async-start(), calls=%async_computation.3 | async-start | bytes 2949120 | tf_op jit(solution)/shard_map/all_gather | solution.py:55
  33.2 99.4 %reduce-scatter.2.cloned.1.call-start = ((), (), s32[]{:S(2)}) async-start(), calls=%async_computation.4 | async-start | bytes 2949120 | tf_op jit(solution)/shard_map/reduce_scatter | solution.py:56
  62.4 9.8 %copy-start.1 = (bf16[320,4096]{1,0:T(8,128)(2,1)S(1)}, bf16[320,4096]{1,0:T(8,128)(2,1)}, u32[]{:S(2)}) copy-start(bf16[320,4096]{1,0:T(8,128)(2,1)} %all-gather.2.cloned.1.call-done) | copy-start | bytes 7864324
  62.4 20.2 %slice-start = ((s8[14680064]{0:T(1024)(128)(4,1)}), s8[4194304]{0:T(1024)(128)(4,1)S(1)}, s32[]{:S(2)}) async-start(s8[14680064]{0:T(1024)(128)(4,1)} %bitcast.38), calls=%async_computation.5 | async-start | bytes 8388608
  62.4 20.2 %slice-start.1 = ((s8[14680064]{0:T(1024)(128)(4,1)}), s8[4194304]{0:T(1024)(128)(4,1)S(1)}, s32[]{:S(2)}) async-start(s8[14680064]{0:T(1024)(128)(4,1)} %bitcast.38), calls=%async_computation.6 | async-start | bytes 8388608
  72.2 10.4 %slice-start.2 = ((s8[14680064]{0:T(1024)(128)(4,1)}), s8[4194304]{0:T(1024)(128)(4,1)S(1)}, s32[]{:S(2)}) async-start(s8[14680064]{0:T(1024)(128)(4,1)} %bitcast.38), calls=%async_computation.7 | async-start | bytes 8388608
  72.2 10.4 %slice-start.3 = ((s8[14680064]{0:T(1024)(128)(4,1)}), s8[2097152]{0:T(1024)(128)(4,1)S(1)}, s32[]{:S(2)}) async-start(s8[14680064]{0:T(1024)(128)(4,1)} %bitcast.38), calls=%async_computation.8 | async-start | bytes 4194304
  88.9 0.7 copy-start
  88.9 50.3 %copy-start.2 = (s32[16]{0:T(128)S(1)}, s32[16]{0:T(128)}, u32[]{:S(2)}) copy-start(s32[16]{0:T(128)} %param.10) | copy-start | bytes 196
  134.4 18.9 %all-to-all-start.1 = ((bf16[4,10,4096]{2,1,0:T(8,128)(2,1)}), bf16[4,10,4096]{2,1,0:T(8,128)(2,1)S(1)}, u32[]{:S(2)}, u32[]{:S(2)}) async-start(bf16[4,10,4096]{2,1,0:T(8,128)(2,1)} %reshape.159), calls=%async_computation.2 | async-start | bytes 1048576 | tf_op jit(solution)/shard_map/all_to_all | solution.py:63
Sparse Core Ops, SparseCore 0:
  33.3 29.0 all-gather.1
  89.1 43.4 reduce-scatter.1
where the time goes:
time: 163 us; the launch traced here: 162 us
  waiting for transfers between devices  86.1 us (53%)
  matrix products  26.4 us (16%)
  blocking collectives  20.6 us (13%)
  between operations  13.6 us (8%)
  local copies, waits for them, and re-layouts  6.62 us (4%)
  starting transfers between devices  4.65 us (3%)
  other arithmetic  4.31 us (3%)
    reduce_scatter x1, waiting for transfers between devices, body(): lax.psum_scatter(jnp.dot(hidden, down_matrix, preferred_element_type=jnp....  42.8 us
    all_gather x1, waiting for transfers between devices, body(): lax.all_gather(received, 'mp', axis=0, tiled=True)  29.2 us
    all_to_all x1, blocking collectives, body(): lax.all_to_all(outgoing.reshape(groups, capacity, model_width), 'expert',...  20.6 us
    all_to_all x1, waiting for transfers between devices, body(): lax.all_to_all(outcome, 'expert', split_axis=0, concat_axis=0, tiled=True)  14.1 us
    dot_general x1, matrix products, swiglu(): up_proj = jnp.dot(row_block, up_matrix, preferred_element_type=jnp.float32)  10.4 us
    dot_general x1, matrix products, swiglu(): jnp.dot(row_block, gate_matrix, preferred_element_type=jnp.float32)  9.74 us
    dot_general x1, matrix products, body(): jnp.dot(hidden, down_matrix, preferred_element_type=jnp.float32)  6.25 us
    all_to_all x1, starting transfers between devices, body(): lax.all_to_all(outcome, 'expert', split_axis=0, concat_axis=0, tiled=True)  4.6 us
  transfers between devices with their start and end apart: 3, of which 3 were waited for; matrix products, arithmetic and copies ran while one was open for 0% of the time, Pallas kernels for 0%

commit v1 on v0

--- a/solution.py
+++ b/solution.py
@@ -1,6 +1,10 @@
+import functools
+
 import jax
 import jax.numpy as jnp
 from jax import lax
+from jax.experimental import pallas as pl
+from jax.experimental.pallas import tpu as pltpu
 from jax.sharding import PartitionSpec as P
 
 DENOM = 1024
@@ -74,6 +78,336 @@
     return mixed_out.astype(jnp.bfloat16)
 
 
+MESH = pl.DeviceIdType.MESH
+F32, BF16 = jnp.float32, jnp.bfloat16
+
+
+def fused_kernel(plan, tok, gain, meta, wg_hbm, wu_hbm, wd_hbm, out,
+                 wg, wu, wd, xbuf, acc_g, acc_u, hidden, nbuf, norm_all, meta_all,
+                 zsend, zrecv, psend, prcv, sums, r1, s2, r2, rsend, zret, mixbuf, orecv,
+                 w_sem, wd_sem, n_sem, m_sem, ml_sem, z_ss, z_rs, x_ss, x_rs, y_ss, y_rs, f_ss, f_rs,
+                 d_ss, d_rs, p_ss, p_rs, a_ss, a_rs, b_ss, b_rs, q_ss, q_rs, o_ss, o_rs):
+    S, CW, groups, cap, stride, tile = plan
+    toks, width = tok.shape
+    half = width // 2
+    rows = groups * cap
+    ff = hidden.shape[1]
+    myz = lax.axis_index("expert")
+    mp = lax.axis_index("mp")
+    core = mp % 2
+    other = 1 - core
+    k = mp // 2
+    kx = k + 1 - 2 * (k % 2)
+    ky = k + 2 - 4 * (k // 2)
+    kd = 3 - k
+    partner = {"mp": 2 * k + other}
+    xn = {"mp": 2 * kx + core}
+    yn = {"mp": 2 * ky + core}
+    zs = [lax.rem(myz + d, groups) for d in range(groups)]
+
+    def remote(src, dst, ss, rs, dev):
+        return pltpu.make_async_remote_copy(src_ref=src, dst_ref=dst, send_sem=ss, recv_sem=rs,
+                                            device_id=dev, device_id_type=MESH)
+
+    barrier = pltpu.get_barrier_semaphore()
+    peers = [partner, xn, yn] + [{"expert": zs[d]} for d in range(1, groups)]
+    for dev in peers:
+        pl.semaphore_signal(barrier, inc=1, device_id=dev, device_id_type=MESH)
+
+    order = []
+    for j in range(S):
+        order += [core * S + j, other * S + j]
+
+    def w_copies(c):
+        at = pl.ds(pl.multiple_of(c * CW, CW), CW)
+        return (pltpu.make_async_copy(wg_hbm.at[0, at, :], wg.at[at, :], w_sem.at[0, c]),
+                pltpu.make_async_copy(wu_hbm.at[0, at, :], wu.at[at, :], w_sem.at[1, c]))
+
+    def wd_copy(c):
+        at = pl.ds(pl.multiple_of(c * CW, CW), CW)
+        return pltpu.make_async_copy(wd_hbm.at[0, :, at], wd.at[:, at], wd_sem.at[c])
+
+    meta_local = pltpu.make_async_copy(meta, meta_all.at[core], ml_sem)
+    meta_local.start()
+    for c in order:
+        for copy in w_copies(c):
+            copy.start()
+    for j in range(S):
+        wd_copy(other * S + j).start()
+        wd_copy(core * S + j).start()
+
+    values = tok[...].astype(F32)
+    inverse = lax.rsqrt(jnp.mean(values * values, axis=1, keepdims=True) + 1e-05)
+    normed = (values * inverse * gain[...].astype(F32)).astype(BF16)
+    nbuf[0] = normed[:, :half]
+    nbuf[1] = normed[:, half:]
+    pl.semaphore_wait(barrier, len(peers))
+    meta_copy = remote(meta, meta_all.at[core], m_sem.at[0], m_sem.at[1], partner)
+    meta_copy.start()
+    norm_copy = remote(nbuf.at[other], norm_all.at[core], n_sem.at[0], n_sem.at[1], partner)
+    norm_copy.start()
+    norm_all[core] = nbuf[core]
+
+    meta_local.wait()
+    meta_copy.wait_recv()
+    info = meta_all[...].reshape(2 * toks, meta.shape[1])
+    id0, id1, num = info[:, 0:1], info[:, 1:2], info[:, 2:3]
+    lanes = lax.broadcasted_iota(jnp.int32, (2 * toks, 128), 1)
+    oh0 = jnp.where(lanes == id0, 1.0, 0.0)
+    oh1 = jnp.where(lanes == id1, 1.0, 0.0)
+    tri_r = lax.broadcasted_iota(jnp.int32, (2 * toks, 2 * toks), 0)
+    tri_c = lax.broadcasted_iota(jnp.int32, (2 * toks, 2 * toks), 1)
+    tri = jnp.where(tri_c < tri_r, 1.0, 0.0).astype(BF16)
+    cnt = jnp.dot(tri, (oh0 + oh1).astype(BF16), preferred_element_type=F32)
+    lane_f = lanes.astype(F32)
+    t0 = id0.astype(F32) * stride + jnp.sum(oh0 * cnt, axis=1, keepdims=True)
+    t1 = id1.astype(F32) * stride + jnp.sum(oh1 * cnt, axis=1, keepdims=True)
+    hit0, hit1 = lane_f == t0, lane_f == t1
+    pick = jnp.where(hit0 | hit1, 1.0, 0.0)
+    pick_t = jnp.transpose(pick).astype(BF16)
+    low0 = num % 4
+    low1 = (DENOM - num) % 4
+    hi = jnp.where(hit0, (num - low0).astype(F32), jnp.where(hit1, (DENOM - num - low1).astype(F32), 0.0))
+    lo = jnp.where(hit0, low0.astype(F32), jnp.where(hit1, low1.astype(F32), 0.0))
+    mix = (jnp.concatenate([hi, lo], axis=0) * (1.0 / DENOM)).astype(BF16)
+
+    norm_copy.wait_recv()
+
+    def z_copy(j, d):
+        return remote(zsend.at[j, zs[d]], zrecv.at[j, myz], z_ss.at[j, d], z_rs.at[j, d], {"expert": zs[d]})
+
+    for j in range(S):
+        block = norm_all[:, :, j * CW:(j + 1) * CW].reshape(2 * toks, CW)
+        picked = jnp.dot(pick_t, block, preferred_element_type=F32).astype(BF16)
+        for z in range(groups):
+            zsend[j, z] = picked[z * stride:z * stride + cap]
+        for d in range(1, groups):
+            z_copy(j, d).start()
+        zrecv[j, myz] = zsend[j, myz]
+
+    acc_g[...] = jnp.zeros_like(acc_g)
+    acc_u[...] = jnp.zeros_like(acc_u)
+
+    def place(z):
+        r = lax.broadcasted_iota(jnp.int32, (rows, cap), 0)
+        c = lax.broadcasted_iota(jnp.int32, (rows, cap), 1)
+        return jnp.where(r == c + z * cap, 1.0, 0.0).astype(BF16)
+
+    def take(z):
+        r = lax.broadcasted_iota(jnp.int32, (cap, rows), 0)
+        c = lax.broadcasted_iota(jnp.int32, (cap, rows), 1)
+        return jnp.where(c == r + z * cap, 1.0, 0.0).astype(BF16)
+
+    def slot(j, who, core_of=core):
+        return xbuf.at[core_of * S + j, who]
+
+    def x_copy(j, who=None):
+        return remote(slot(j, k), slot(j, k), x_ss.at[j], x_rs.at[j], xn)
+
+    def y_copy(j):
+        return remote(slot(j, k), slot(j, k), y_ss.at[j], y_rs.at[j], yn)
+
+    def f_copy(j):
+        if j % 2 == 0:
+            return remote(slot(j, kx), slot(j, kx), f_ss.at[j], f_rs.at[j], yn)
+        return remote(slot(j, ky), slot(j, ky), f_ss.at[j], f_rs.at[j], xn)
+
+    whos = (k, kx, ky, kd)
+
+    def d_copy(j, i):
+        return remote(slot(j, whos[i]), slot(j, whos[i]), d_ss.at[j, i], d_rs.at[j, i], partner)
+
+    def stage_c(j):
+        total = jnp.zeros((rows, CW), F32)
+        for d in range(1, groups):
+            z_copy(j, d).wait_recv()
+        for z in range(groups):
+            total = total + jnp.dot(place(z), zrecv[j, z], preferred_element_type=F32)
+        xbuf[core * S + j, k] = total.astype(BF16)
+        x_copy(j).start()
+        y_copy(j).start()
+        d_copy(j, 0).start()
+
+    def stage_d(j):
+        x_copy(j).wait_recv()
+        if j % 2 == 0:
+            f_copy(j).start()
+        d_copy(j, 1).start()
+        y_copy(j).wait_recv()
+        if j % 2 == 1:
+            f_copy(j).start()
+        d_copy(j, 2).start()
+
+    def up_mm(c, last):
+        for copy in w_copies(c):
+            copy.wait()
+        at = pl.ds(pl.multiple_of(c * CW, CW), CW)
+
+        def step(n, carry):
+            cols = pl.ds(pl.multiple_of(n * tile, tile), tile)
+            x = xbuf[c].reshape(4 * rows, CW)
+            g = acc_g[:, cols] + jnp.dot(x, wg[at, cols], preferred_element_type=F32)
+            u = acc_u[:, cols] + jnp.dot(x, wu[at, cols], preferred_element_type=F32)
+            if last:
+                hidden[:, cols] = (g / (1.0 + jnp.exp(-g)) * u).astype(BF16)
+            else:
+                acc_g[:, cols] = g
+                acc_u[:, cols] = u
+            return carry
+
+        lax.fori_loop(0, ff // tile, step, 0)
+
+    def stage_e(j):
+        f_copy(j).wait_recv()
+        d_copy(j, 3).start()
+        up_mm(core * S + j, False)
+        for i in range(4):
+            d_copy(j, i).wait_recv()
+        up_mm(other * S + j, j == S - 1)
+
+    ahead = max(1, S // 4)
+    for j in range(S):
+        stage_c(j)
+    for j in range(S + ahead):
+        if j < S:
+            stage_d(j)
+        if j >= ahead:
+            stage_e(j - ahead)
+
+    def down(c):
+        at = pl.ds(pl.multiple_of(c * CW, CW), CW)
+        wd_copy(c).wait()
+        return jnp.dot(hidden[...], wd[:, at], preferred_element_type=F32)
+
+    def p_copy(j):
+        return remote(psend.at[j], prcv.at[j], p_ss.at[j], p_rs.at[j], partner)
+
+    def near(j):
+        return (kx, ky, xn, yn) if j % 2 == 0 else (ky, kx, yn, xn)
+
+    def a_copy(j, i):
+        first, _, dev, _ = near(j)
+        return remote(sums.at[j, (first, kd)[i]], r1.at[j, i], a_ss.at[j, i], a_rs.at[j, i], dev)
+
+    def b_copy(j):
+        return remote(s2.at[j], r2.at[j], b_ss.at[j], b_rs.at[j], near(j)[3])
+
+    def stage_0a(j):
+        psend[j] = down(other * S + j).astype(BF16).reshape(4, rows, CW)
+        p_copy(j).start()
+
+    def stage_0(j):
+        own = down(core * S + j).reshape(4, rows, CW)
+        p_copy(j).wait_recv()
+        sums[j] = (own + prcv[j].astype(F32)).astype(BF16)
+        a_copy(j, 1).start()
+        a_copy(j, 0).start()
+
+    def stage_2(j):
+        a_copy(j, 1).wait_recv()
+        s2[j] = (sums[j, near(j)[1]].astype(F32) + r1[j, 1].astype(F32)).astype(BF16)
+        b_copy(j).start()
+
+    def q_copy(j, d):
+        return remote(rsend.at[j, zs[d]], zret.at[j, myz], q_ss.at[j, d], q_rs.at[j, d], {"expert": zs[d]})
+
+    def stage_3(j):
+        a_copy(j, 0).wait_recv()
+        b_copy(j).wait_recv()
+        fin = (sums[j, k].astype(F32) + r1[j, 0].astype(F32) + r2[j].astype(F32)).astype(BF16)
+        for z in range(groups):
+            rsend[j, z] = jnp.dot(take(z), fin, preferred_element_type=F32).astype(BF16)
+        for d in range(1, groups):
+            q_copy(j, d).start()
+        zret[j, myz] = rsend[j, myz]
+
+    def o_copy(j):
+        return remote(mixbuf.at[j, other], orecv.at[j], o_ss.at[j], o_rs.at[j], partner)
+
+    def stage_4(j):
+        for d in range(1, groups):
+            q_copy(j, d).wait_recv()
+        total = jnp.zeros((4 * toks, CW), F32)
+        for z in range(groups):
+            total = total + jnp.dot(mix[:, z * stride:z * stride + cap], zret[j, z], preferred_element_type=F32)
+        mixed = (total[:2 * toks] + total[2 * toks:]).astype(BF16)
+        mixbuf[j] = mixed.reshape(2, toks, CW)
+        o_copy(j).start()
+        out[:, pl.ds(pl.multiple_of((core * S + j) * CW, CW), CW)] = mixbuf[j, core]
+
+    stage_0a(0)
+    for j in range(S):
+        if j + 1 < S:
+            stage_0a(j + 1)
+        stage_0(j)
+    for j in range(S):
+        stage_2(j)
+    for j in range(S + 1):
+        if j < S:
+            stage_3(j)
+        if j >= 1:
+            stage_4(j - 1)
+    for j in range(S):
+        o_copy(j).wait_recv()
+        out[:, pl.ds(pl.multiple_of((other * S + j) * CW, CW), CW)] = orecv[j]
+
+    meta_copy.wait_send()
+    norm_copy.wait_send()
+    for j in range(S):
+        for d in range(1, groups):
+            z_copy(j, d).wait_send()
+            q_copy(j, d).wait_send()
+        for copy in (x_copy(j), y_copy(j), f_copy(j), p_copy(j), a_copy(j, 0), a_copy(j, 1), b_copy(j), o_copy(j)):
+            copy.wait_send()
+        for i in range(4):
+            d_copy(j, i).wait_send()
+
+
+def fused_body(tokens, gain, expert_ids, gate_num, w_gate, w_up, w_down):
+    groups = lax.axis_size("expert")
+    toks, width = tokens.shape
+    ff = w_gate.shape[2]
+    cap = 2 * ((5 * toks * expert_ids.shape[1] + 4 * groups - 1) // (4 * groups))
+    stride = -(-cap // 16) * 16
+    rows = groups * cap
+    S = SPLIT
+    CW = width // 2 // S
+    meta = jnp.concatenate([expert_ids, gate_num[:, None]], axis=1)
+    dma = pltpu.SemaphoreType.DMA
+    vm = pltpu.VMEM
+    scratch = [
+        vm((width, ff), BF16), vm((width, ff), BF16), vm((ff, width), BF16),
+        vm((2 * S, 4, rows, CW), BF16), vm((4 * rows, ff), F32), vm((4 * rows, ff), F32), vm((4 * rows, ff), BF16),
+        vm((2, toks, width // 2), BF16), vm((2, toks, width // 2), BF16), vm((2, toks, 3), jnp.int32),
+        vm((S, groups, cap, CW), BF16), vm((S, groups, cap, CW), BF16),
+        vm((S, 4, rows, CW), BF16), vm((S, 4, rows, CW), BF16), vm((S, 4, rows, CW), BF16),
+        vm((S, 2, rows, CW), BF16), vm((S, rows, CW), BF16), vm((S, rows, CW), BF16),
+        vm((S, groups, cap, CW), BF16), vm((S, groups, cap, CW), BF16),
+        vm((S, 2, toks, CW), BF16), vm((S, toks, CW), BF16),
+        dma((2, 2 * S)), dma((2 * S,)), dma((2,)), dma((2,)), dma,
+        dma((S, groups)), dma((S, groups)), dma((S,)), dma((S,)), dma((S,)), dma((S,)), dma((S,)), dma((S,)),
+        dma((S, 4)), dma((S, 4)), dma((S,)), dma((S,)), dma((S, 2)), dma((S, 2)), dma((S,)), dma((S,)),
+        dma((S, groups)), dma((S, groups)), dma((S,)), dma((S,)),
+    ]
+    inside, outside = pl.BlockSpec(memory_space=pltpu.VMEM), pl.BlockSpec(memory_space=pl.ANY)
+    tile = 256 if ff % 256 == 0 else 128
+    return pl.pallas_call(
+        functools.partial(fused_kernel, (S, CW, groups, cap, stride, tile)),
+        out_shape=jax.ShapeDtypeStruct((toks, width), BF16),
+        in_specs=[inside] * 3 + [outside] * 3,
+        out_specs=inside,
+        scratch_shapes=scratch,
+        compiler_params=pltpu.CompilerParams(collective_id=0, has_side_effects=True, vmem_limit_bytes=67043328),
+    )(tokens, gain.reshape(1, width), meta, w_gate, w_up, w_down)
+
+
+SPLIT = 4
+
+
+def fits(mesh):
+    return mesh.shape["mp"] == 8 and mesh.shape["expert"] <= 4
+
+
 def solution(mesh):
     in_specs = (
         P(("expert", "mp"), None),
@@ -85,4 +419,4 @@
         P("expert", "mp", None),
     )
     out_specs = P(("expert", "mp"), None)
-    return jax.shard_map(body, mesh=mesh, in_specs=in_specs, out_specs=out_specs, check_vma=False)
+    return jax.shard_map(fused_body if fits(mesh) else body, mesh=mesh, in_specs=in_specs, out_specs=out_specs, check_vma=False)

time: 163 us -> 77.4 us (0.47)
  waiting for transfers between devices: 86.1 us -> 0 us
  Pallas kernels: 0 us -> 72.9 us
  matrix products: 26.4 us -> 0 us
  blocking collectives: 20.6 us -> 0 us
  between operations: 13.6 us -> 0.01 us
  starting transfers between devices: 4.65 us -> 0 us
  other arithmetic: 4.31 us -> 0.7 us
  local copies, waits for them, and re-layouts: 6.62 us -> 3.56 us
    pallas_call x0 -> x1, Pallas kernels: none -> 72.9 us  [fused_body(): pl.pallas_call(functools.partial(fused_kernel, (S, CW, groups, cap, strid...]
    reduce_scatter x1 -> x0, waiting for transfers between devices: 42.8 us -> none  [body(): lax.psum_scatter(jnp.dot(hidden, down_matrix, preferred_element_type=jnp....]
    all_gather x1 -> x0, waiting for transfers between devices: 29.2 us -> none  [body(): lax.all_gather(received, 'mp', axis=0, tiled=True)]
    dot_general x3 -> x0, matrix products: 26.4 us -> none  [the longest x1 10.4 us: swiglu(): up_proj = jnp.dot(row_block, up_matrix, preferred_element_type=jnp.float32)]
    all_to_all x1 -> x0, blocking collectives: 20.6 us -> none  [body(): lax.all_to_all(outgoing.reshape(groups, capacity, model_width), 'expert',...]
    all_to_all x1 -> x0, waiting for transfers between devices: 14.1 us -> none  [body(): lax.all_to_all(outcome, 'expert', split_axis=0, concat_axis=0, tiled=True)]
    all_to_all x1 -> x0, starting transfers between devices: 4.6 us -> none  [body(): lax.all_to_all(outcome, 'expert', split_axis=0, concat_axis=0, tiled=True)]
    convert_element_type x4 -> x0, other arithmetic: 2.78 us -> none  [the longest x2 1.71 us: rms_normed(): return (values * inverse * gain.astype(jnp.float32)).astype(jnp.bfloat16)]
  transfers between devices with their start and end apart: 3 -> 0, of which waited for: 3 -> 0; matrix products, arithmetic and copies ran while one was open for 0% -> 0% of each run, Pallas kernels for 0% -> 0%
where the time goes in v1:
time: 77.4 us; the launch traced here: 77.1 us
  Pallas kernels  72.9 us (94%)
  local copies, waits for them, and re-layouts  3.56 us (5%)
    pallas_call x1, Pallas kernels, fused_body(): pl.pallas_call(functools.partial(fused_kernel, (S, CW, groups, cap, strid...  72.9 us
    unnamed x1, local copies, waits for them, and re-layouts  1.57 us

profile of v1, /device:TPU:0, one launch (start us, length us, event | category | flops | bytes accessed | tf_op | source)
XLA Modules:
  0.0 77.1 jit_solution(3725942626245509741)
XLA Ops:
  0.0 0.7 pad_add_fusion
  0.7 0.7 copy.10.meta
  1.4 1.3 %reshape.3.gain = bf16[1,4096]{1,0:T(2,128)(2,1)} reshape(bf16[4096]{0:T(1024)(128)(2,1)} %param.8) | data formatting | bytes 16384 | tf_op jit(solution)/shard_map/reshape | solution.py:401
  2.7 72.9 %shard_map.73 = bf16[16,4096]{1,0:T(8,128)(2,1)} custom-call(bf16[16,4096]{1,0:T(8,128)(2,1)} %tok.1, bf16[1,4096]{1,0:T(2,128)(2,1)} %reshape.3.gain, s32[16,3]{1,0:T(8,128)} %copy.10.meta, bf16[1,4096,1792]{2,1,0:T(8,128)(2,1)} %wg_hbm.1, bf16[1,4096,1792]{2,1,0:T(8,128)(2,1)} %wu_hbm.1, bf16[1,1792,4096]{2,1,0:T(8,128)(2,1)} %wd_hbm.1), custom_call_target="tpu_custom_call" | custom-call | tf_op jit(solution)/shard_map/pallas_call | solution.py:394
  75.6 1.6 %copy.12 = bf16[16,4096]{1,0:T(8,128)(2,1)} copy(bf16[16,4096]{1,0:T(8,128)(2,1)} %shard_map.73) | data formatting | bytes 262144

commit v2 on v1

--- a/solution.py
+++ b/solution.py
@@ -82,10 +82,11 @@
 F32, BF16 = jnp.float32, jnp.bfloat16
 
 
-def fused_kernel(plan, tok, gain, meta, wg_hbm, wu_hbm, wd_hbm, out,
-                 wg, wu, wd, xbuf, acc_g, acc_u, hidden, nbuf, norm_all, meta_all,
+def fused_kernel(plan, tok_hbm, gain_hbm, ids_hbm, num_hbm, wg_hbm, wu_hbm, wd_hbm, out,
+                 tok, gain, ids_loc, num_loc, ids_all, num_all, pad, i_sem, out_sem,
+                 wg, wu, wd, xbuf, acc_g, acc_u, hidden, nbuf, norm_all,
                  zsend, zrecv, psend, prcv, sums, r1, s2, r2, rsend, zret, mixbuf, orecv,
-                 w_sem, wd_sem, n_sem, m_sem, ml_sem, z_ss, z_rs, x_ss, x_rs, y_ss, y_rs, f_ss, f_rs,
+                 w_sem, wd_sem, n_sem, m_sem, z_ss, z_rs, x_ss, x_rs, y_ss, y_rs, f_ss, f_rs,
                  d_ss, d_rs, p_ss, p_rs, a_ss, a_rs, b_ss, b_rs, q_ss, q_rs, o_ss, o_rs):
     S, CW, groups, cap, stride, tile = plan
     toks, width = tok.shape
@@ -127,30 +128,44 @@
         at = pl.ds(pl.multiple_of(c * CW, CW), CW)
         return pltpu.make_async_copy(wd_hbm.at[0, :, at], wd.at[:, at], wd_sem.at[c])
 
-    meta_local = pltpu.make_async_copy(meta, meta_all.at[core], ml_sem)
-    meta_local.start()
+    entries = [pltpu.make_async_copy(a, b, i_sem.at[i]) for i, (a, b) in enumerate(
+        ((tok_hbm, tok), (gain_hbm, gain), (ids_hbm, ids_loc), (num_hbm, num_loc)))]
+    for copy in entries:
+        copy.start()
+
+    pad[...] = jnp.zeros_like(pad)
+    for copy in entries:
+        copy.wait()
     for c in order:
         for copy in w_copies(c):
             copy.start()
     for j in range(S):
         wd_copy(other * S + j).start()
         wd_copy(core * S + j).start()
-
+    ids_all[core] = ids_loc[...]
+    num_all[core] = num_loc[...]
     values = tok[...].astype(F32)
     inverse = lax.rsqrt(jnp.mean(values * values, axis=1, keepdims=True) + 1e-05)
-    normed = (values * inverse * gain[...].astype(F32)).astype(BF16)
-    nbuf[0] = normed[:, :half]
-    nbuf[1] = normed[:, half:]
+    gains = gain[...].astype(F32)
+    for r in range(width // 128):
+        part = values[:, r * 128:(r + 1) * 128] * inverse * gains[r:r + 1]
+        at = r * 128 % half
+        nbuf[r * 128 // half, :, at:at + 128] = part.astype(BF16)
     pl.semaphore_wait(barrier, len(peers))
-    meta_copy = remote(meta, meta_all.at[core], m_sem.at[0], m_sem.at[1], partner)
-    meta_copy.start()
+    ids_copy = remote(ids_loc, ids_all.at[core], m_sem.at[0], m_sem.at[1], partner)
+    num_copy = remote(num_loc, num_all.at[core], m_sem.at[2], m_sem.at[3], partner)
+    ids_copy.start()
+    num_copy.start()
     norm_copy = remote(nbuf.at[other], norm_all.at[core], n_sem.at[0], n_sem.at[1], partner)
     norm_copy.start()
     norm_all[core] = nbuf[core]
 
-    meta_local.wait()
-    meta_copy.wait_recv()
-    info = meta_all[...].reshape(2 * toks, meta.shape[1])
+    ids_copy.wait_recv()
+    num_copy.wait_recv()
+    for c in range(2):
+        pad[c, 0:2, 0:toks] = ids_all[c].astype(F32)
+        pad[c, 2:3, 0:toks] = num_all[c].astype(F32)
+    info = jnp.concatenate([jnp.transpose(pad[c])[:toks] for c in range(2)], axis=0).astype(jnp.int32)
     id0, id1, num = info[:, 0:1], info[:, 1:2], info[:, 2:3]
     lanes = lax.broadcasted_iota(jnp.int32, (2 * toks, 128), 1)
     oh0 = jnp.where(lanes == id0, 1.0, 0.0)
@@ -258,21 +273,29 @@
         lax.fori_loop(0, ff // tile, step, 0)
 
     def stage_e(j):
+        stage_e1(j)
+        stage_e2(j)
+
+    def stage_e1(j):
         f_copy(j).wait_recv()
         d_copy(j, 3).start()
         up_mm(core * S + j, False)
+
+    def stage_e2(j):
         for i in range(4):
             d_copy(j, i).wait_recv()
         up_mm(other * S + j, j == S - 1)
 
-    ahead = max(1, S // 4)
-    for j in range(S):
+    stage_c(0)
+    for j in range(1, S):
         stage_c(j)
-    for j in range(S + ahead):
-        if j < S:
-            stage_d(j)
-        if j >= ahead:
-            stage_e(j - ahead)
+        stage_d(j - 1)
+        if j >= 2:
+            stage_e(j - 2)
+    stage_e1(S - 2)
+    stage_d(S - 1)
+    stage_e2(S - 2)
+    stage_e(S - 1)
 
     def down(c):
         at = pl.ds(pl.multiple_of(c * CW, CW), CW)
@@ -300,6 +323,8 @@
         own = down(core * S + j).reshape(4, rows, CW)
         p_copy(j).wait_recv()
         sums[j] = (own + prcv[j].astype(F32)).astype(BF16)
+
+    def stage_1(j):
         a_copy(j, 1).start()
         a_copy(j, 0).start()
 
@@ -333,25 +358,35 @@
         mixed = (total[:2 * toks] + total[2 * toks:]).astype(BF16)
         mixbuf[j] = mixed.reshape(2, toks, CW)
         o_copy(j).start()
-        out[:, pl.ds(pl.multiple_of((core * S + j) * CW, CW), CW)] = mixbuf[j, core]
+        out_copy(j, 0).start()
+
+    def out_copy(j, i):
+        cols = pl.ds(pl.multiple_of(((core, other)[i] * S + j) * CW, CW), CW)
+        return pltpu.make_async_copy((mixbuf.at[j, core], orecv.at[j])[i], out.at[:, cols], out_sem.at[j, i])
 
     stage_0a(0)
     for j in range(S):
         if j + 1 < S:
             stage_0a(j + 1)
         stage_0(j)
-    for j in range(S):
+        if j < 2:
+            stage_1(j)
+    for j in range(0, S, 2):
         stage_2(j)
-    for j in range(S + 1):
-        if j < S:
-            stage_3(j)
-        if j >= 1:
-            stage_4(j - 1)
+        stage_2(j + 1)
+        if j + 2 < S:
+            stage_1(j + 2)
+            stage_1(j + 3)
+        stage_3(j)
+        stage_3(j + 1)
+    for j in range(S):
+        stage_4(j)
     for j in range(S):
         o_copy(j).wait_recv()
-        out[:, pl.ds(pl.multiple_of((other * S + j) * CW, CW), CW)] = orecv[j]
-
-    meta_copy.wait_send()
+        out_copy(j, 1).start()
+
+    ids_copy.wait_send()
+    num_copy.wait_send()
     norm_copy.wait_send()
     for j in range(S):
         for d in range(1, groups):
@@ -361,6 +396,8 @@
             copy.wait_send()
         for i in range(4):
             d_copy(j, i).wait_send()
+        out_copy(j, 0).wait()
+        out_copy(j, 1).wait()
 
 
 def fused_body(tokens, gain, expert_ids, gate_num, w_gate, w_up, w_down):
@@ -372,33 +409,34 @@
     rows = groups * cap
     S = SPLIT
     CW = width // 2 // S
-    meta = jnp.concatenate([expert_ids, gate_num[:, None]], axis=1)
     dma = pltpu.SemaphoreType.DMA
     vm = pltpu.VMEM
     scratch = [
+        vm((toks, width), BF16), vm((width // 128, 128), BF16), vm((2, toks), jnp.int32), vm((1, toks), jnp.int32),
+        vm((2, 2, toks), jnp.int32), vm((2, 1, toks), jnp.int32), vm((2, 8, 128), F32), dma((4,)), dma((S, 2)),
         vm((width, ff), BF16), vm((width, ff), BF16), vm((ff, width), BF16),
         vm((2 * S, 4, rows, CW), BF16), vm((4 * rows, ff), F32), vm((4 * rows, ff), F32), vm((4 * rows, ff), BF16),
-        vm((2, toks, width // 2), BF16), vm((2, toks, width // 2), BF16), vm((2, toks, 3), jnp.int32),
+        vm((2, toks, width // 2), BF16), vm((2, toks, width // 2), BF16),
         vm((S, groups, cap, CW), BF16), vm((S, groups, cap, CW), BF16),
         vm((S, 4, rows, CW), BF16), vm((S, 4, rows, CW), BF16), vm((S, 4, rows, CW), BF16),
         vm((S, 2, rows, CW), BF16), vm((S, rows, CW), BF16), vm((S, rows, CW), BF16),
         vm((S, groups, cap, CW), BF16), vm((S, groups, cap, CW), BF16),
         vm((S, 2, toks, CW), BF16), vm((S, toks, CW), BF16),
-        dma((2, 2 * S)), dma((2 * S,)), dma((2,)), dma((2,)), dma,
+        dma((2, 2 * S)), dma((2 * S,)), dma((2,)), dma((4,)),
         dma((S, groups)), dma((S, groups)), dma((S,)), dma((S,)), dma((S,)), dma((S,)), dma((S,)), dma((S,)),
         dma((S, 4)), dma((S, 4)), dma((S,)), dma((S,)), dma((S, 2)), dma((S, 2)), dma((S,)), dma((S,)),
         dma((S, groups)), dma((S, groups)), dma((S,)), dma((S,)),
     ]
-    inside, outside = pl.BlockSpec(memory_space=pltpu.VMEM), pl.BlockSpec(memory_space=pl.ANY)
+    outside = pl.BlockSpec(memory_space=pl.ANY)
     tile = 256 if ff % 256 == 0 else 128
     return pl.pallas_call(
         functools.partial(fused_kernel, (S, CW, groups, cap, stride, tile)),
         out_shape=jax.ShapeDtypeStruct((toks, width), BF16),
-        in_specs=[inside] * 3 + [outside] * 3,
-        out_specs=inside,
+        in_specs=[outside] * 7,
+        out_specs=outside,
         scratch_shapes=scratch,
         compiler_params=pltpu.CompilerParams(collective_id=0, has_side_effects=True, vmem_limit_bytes=67043328),
-    )(tokens, gain.reshape(1, width), meta, w_gate, w_up, w_down)
+    )(tokens, gain.reshape(width // 128, 128), expert_ids.T, gate_num.reshape(1, toks), w_gate, w_up, w_down)
 
 
 SPLIT = 4

time: 77.4 us -> 67.3 us (0.87)
  Pallas kernels: 72.9 us -> 65.2 us
  local copies, waits for them, and re-layouts: 3.56 us -> 1.57 us
    pallas_call x1, Pallas kernels: 72.9 us -> 65.2 us  [fused_body(): pl.pallas_call(functools.partial(fused_kernel, (S, CW, groups, cap, strid...]
    reshape x1 -> x0, local copies, waits for them, and re-layouts: 1.31 us -> none  [fused_body(): gain.reshape(1, width)]
where the time goes in v2:
time: 67.3 us; the launch traced here: 66.8 us
  Pallas kernels  65.2 us (97%)
  local copies, waits for them, and re-layouts  1.57 us (2%)
    pallas_call x1, Pallas kernels, fused_body(): pl.pallas_call(functools.partial(fused_kernel, (S, CW, groups, cap, strid...  65.2 us
    unnamed x1, local copies, waits for them, and re-layouts  1.57 us

profile of v2, /device:TPU:0, one launch (start us, length us, event | category | flops | bytes accessed | tf_op | source)
XLA Modules:
  0.0 66.8 jit_solution(8731806383694682998)
XLA Ops:
  0.0 65.2 %shard_map.73 = bf16[16,4096]{1,0:T(8,128)(2,1)} custom-call(bf16[16,4096]{1,0:T(8,128)(2,1)} %tok_hbm.1, bf16[32,128]{1,0:T(8,128)(2,1)} %bitcast.3, s32[2,16]{1,0:T(2,128)} %bitcast.4, s32[1,16]{1,0:T(1,128)} %bitcast.5, bf16[1,4096,1792]{2,1,0:T(8,128)(2,1)} %wg_hbm.1, bf16[1,4096,1792]{2,1,0:T(8,128)(2,1)} %wu_hbm.1, bf16[1,1792,4096]{2,1,0:T(8,128)(2,1)} %wd_hbm.1), custom_call_target="tpu_custom_call" | custom-call | tf_op jit(solution)/shard_map/pallas_call | solution.py:432
  65.2 1.6 %copy.9 = bf16[16,4096]{1,0:T(8,128)(2,1)} copy(bf16[16,4096]{1,0:T(8,128)(2,1)} %shard_map.73) | data formatting | bytes 262144
